TPU v7x, 32 devices: a whole 2x2x4 slice. The times are simulated.
32 devices in a mesh: dp: 8 (over z, x), tensor: 4 (over y, core).
Axes of the slice: x: 2, y: 2, z: 4, core: 2. Of those that a mesh axis runs over, the one named last changes fastest.
Arguments:
- out_first: bfloat16 [8, 197, 1024], P('dp', None, 'tensor'), may hold values from -6 to 6
- out_second: bfloat16 [8, 197, 1024], P('dp', None, 'tensor'), may hold values from -6 to 6
- grad_first: bfloat16 [8, 197, 1024], P('dp', None, 'tensor'), may hold values from -6 to 6
- grad_second: bfloat16 [8, 197, 1024], P('dp', None, 'tensor'), may hold values from -6 to 6
- gain_attn: float32 [1024], replicated, may hold values from 0.25 to 1.75
- gain_mlp: float32 [1024], replicated, may hold values from 0.25 to 1.75
- qkv_weight: bfloat16 [1024, 3, 1024], P(None, None, 'tensor'), may hold values from -1 to 1
- proj_weight: bfloat16 [1024, 1024], P(None, 'tensor'), may hold values from -0.1875 to 0.1875
- inner_weight: bfloat16 [1024, 4096], P(None, 'tensor'), may hold values from -0.1875 to 0.1875
- inner_bias: float32 [4096], P('tensor'), may hold values from -3 to 3
- outer_weight: bfloat16 [1024, 4096], P(None, 'tensor'), may hold values from -0.09375 to 0.09375
Outputs:
- input_first: bfloat16 [8, 197, 1024], P('dp', None, 'tensor')
- input_second: bfloat16 [8, 197, 1024], P('dp', None, 'tensor')
- back_first: bfloat16 [8, 197, 1024], P('dp', None, 'tensor')
- back_second: bfloat16 [8, 197, 1024], P('dp', None, 'tensor')
- grad_qkv: float32 [1024, 3, 1024], P('dp', None, 'tensor')
- grad_proj: float32 [1024, 1024], P('dp', 'tensor')
- grad_inner: float32 [1024, 4096], P('dp', 'tensor')
- grad_bias: float32 [4096], P('tensor')
- grad_outer: float32 [1024, 4096], P('dp', 'tensor')
- grad_gain_attn: float32 [1024], P('tensor')
- grad_gain_mlp: float32 [1024], P('tensor')
All inputs are finite; a program needn't handle non-finite values.
Results may differ from a plain program's by a relative error of at most 0.016.
Values may be sent and summed in bfloat16 or wider, within the bound.
A program may use at most 64 MiB of HBM per device.

v0:
```python
import functools

import jax
import jax.numpy as jnp
from jax import lax
from jax.experimental import pallas as pl
from jax.experimental.pallas import tpu as pltpu
from jax.sharding import PartitionSpec as P

epsilon = 1e-06
HEAD = 64
BF = jnp.bfloat16
F32 = jnp.float32
MESH = pl.DeviceIdType.MESH
LIMIT = 61 * 2**20


def dot(a, b, dims=((1,), (0,))):
    return lax.dot_general(a, b, (dims, ((), ())), preferred_element_type=F32)


NT = ((1,), (1,))
TN = ((0,), (0,))


def kernel(
    sizes,
    of_ref, os_ref, gf_ref, gs_ref, gain_attn, gain_mlp, bias,
    qkv_hbm, proj_hbm, inner_hbm, outer_hbm,
    o_if, o_is, o_bf, o_bs, o_qkv, o_proj, o_inner, o_ga, o_gm, o_bias, o_outer,
    w_qkv, w_proj, w_inner, w_outer,
    g_in, g_gf, g_is, g_gn, g_gna,
    a_mlp, a_more, a_attn, a_back, n_mlp, n_attn, sp_attn,
    dgelu, qkv, gheads,
    at, lr, atm, at_tmp,
    r_act, r_gh, r_attn, r_rows,
    rs_s1, rs_r1, rs_k, rs_s2, rs_r2,
    sm_s, sm_r,
    *rest,
):
    groups, length, width, full, hid, tile, rows = sizes
    bits = groups.bit_length() - 1
    shard = full // groups
    pieces = rest[:-3]
    ssem, rsem, wsem = rest[-3:]
    d = lax.axis_index("dp")
    me = lax.axis_index("tensor")
    core, yy = me % 2, me // 2
    tc = yy * 2 + 1 - core
    ty = (1 - yy) * 2 + core
    td = (1 - yy) * 2 + 1 - core
    bit = [(d // 2**k) % 2 for k in range(bits)]
    partner = [d + (1 - 2 * bit[k]) * 2**k for k in range(bits)]
    counter = [0]
    pending = []

    def send(src, dst, dp_id, t_id):
        k = counter[0]
        counter[0] += 1
        c = pltpu.make_async_remote_copy(
            src_ref=src, dst_ref=dst, send_sem=ssem.at[k], recv_sem=rsem.at[k],
            device_id=(dp_id, t_id), device_id_type=MESH,
        )
        c.start()
        pending.append(c)
        return c

    def cols(i):
        return pl.ds(pl.multiple_of(i * width, width), width)

    weights = []
    for i, (src, dst) in enumerate(
        [(inner_hbm, w_inner), (outer_hbm, w_outer), (qkv_hbm, w_qkv), (proj_hbm, w_proj)]
    ):
        c = pltpu.make_async_copy(src, dst, wsem.at[i])
        c.start()
        weights.append(c)

    barrier = pltpu.get_barrier_semaphore()
    peers = [(d, tc), (d, ty)] + [(p, me) for p in partner]
    for peer in peers:
        pl.semaphore_signal(barrier, inc=1, device_id=peer, device_id_type=MESH)

    def stage(g, src):
        g[:, cols(me)] = jnp.zeros((rows, width), BF)
        g[0:length, cols(me)] = src[0]

    g_of, g_low = g_in.at[0, 0], g_in.at[0, 1]
    stage(g_of, of_ref)
    stage(g_low, gs_ref)
    stage(g_gf, gf_ref)
    pl.semaphore_wait(barrier, len(peers))

    def part_of(g, i):
        return g.at[:, cols(i)] if len(g.shape) == 2 else g.at[:, :, cols(i)]

    def ag_start(g):
        own = part_of(g, me)
        c2 = send(own, own, d, ty)
        c1 = send(own, own, d, tc)
        return [c1, c2]

    def ag_mid(g, cs):
        cs[1].wait_recv()
        far = part_of(g, ty)
        cs.append(send(far, far, d, tc))

    def ag_end(cs):
        cs[0].wait_recv()
        cs[2].wait_recv()

    def rs_start(i, part):
        rs_s1[i, 0] = part(tc).astype(BF)
        c0 = send(rs_s1.at[i, 0], rs_r1.at[i, 0], d, tc)
        rs_s1[i, 1] = part(td).astype(BF)
        c1 = send(rs_s1.at[i, 1], rs_r1.at[i, 1], d, tc)
        rs_k[i, 1] = part(ty)
        rs_k[i, 0] = part(me)
        return [c0, c1]

    def rs_mid(i, cs):
        cs[1].wait_recv()
        rs_s2[i] = (rs_k[i, 1] + rs_r1[i, 1].astype(F32)).astype(BF)
        cs.append(send(rs_s2.at[i], rs_r2.at[i], d, ty))

    def rs_end(i, cs):
        cs[0].wait_recv()
        cs[2].wait_recv()
        return rs_k[i, 0] + rs_r1[i, 0].astype(F32) + rs_r2[i].astype(F32)

    def normalize(values):
        centre = values - jnp.mean(values, -1, keepdims=True)
        spread = lax.rsqrt(jnp.mean(centre * centre, -1, keepdims=True) + epsilon)
        return centre * spread, spread

    def left(i, a):
        t = a[...].T
        at[i] = t.reshape(groups // 2, 2, shard, rows)
        return send(at.at[i, :, 1 - bit[0]], lr.at[i], partner[0], me)

    def right(r):
        return send(r.at[0], r.at[1], partner[0], me)

    def piece(p, i, r, cr):
        cr.wait_recv()
        keep = pieces[p][0]
        m = groups // 2
        mine = at[i, :, bit[0]].reshape(m * shard, rows)
        theirs = lr[i].reshape(m * shard, rows)
        for j in range(r.shape[2] // width):
            c = slice(j * width, (j + 1) * width)
            acc = dot(mine, r[0, :, c]) + dot(theirs, r[1, :, c])
            keep[:, :, :, c] = acc.reshape(m // 2, 2, shard, width)
        return halve(p, 1)

    def keep_left(s, kind, a):
        m = groups // 2
        if shard % 128 == 0:
            for i in range(m):
                at_c = pl.ds(pl.multiple_of((2 * i + bit[0]) * shard, shard), shard)
                atm[s, kind, i] = a[:, at_c].T
        else:
            at_tmp[...] = a[...].T.reshape(m, 2, shard, rows)
            atm[s, kind] = at_tmp[:, bit[0]]

    def mlp_piece(p, kind, r):
        keep = pieces[p][0]
        m = groups // 2
        for j in range(hid // tile):
            c = slice(j * tile, (j + 1) * tile)
            acc = dot(atm[0, kind].reshape(m * shard, rows), r[0, :, c])
            for s in range(1, 2):
                acc = acc + dot(atm[s, kind].reshape(m * shard, rows), r[s, :, c])
            keep[:, :, :, c] = acc.reshape(m // 2, 2, shard, tile)
        return halve(p, 1)

    def bufs(p, k):
        at_k = 3 * (k - 1)
        return pieces[p][at_k : at_k + 3]

    def halve(p, k):
        keep, s, r = bufs(p, k)
        s[...] = keep[:, 1 - bit[k]].astype(BF)
        return send(s, r, partner[k], me)

    def merge(p, k, c):
        c.wait_recv()
        keep, s, r = bufs(p, k)
        total = keep[:, bit[k]] + r[...].astype(F32)
        if k == bits - 1:
            outs[p][...] = total[0]
            return None
        nxt = bufs(p, k + 1)[0]
        nxt[...] = total.reshape(nxt.shape)
        return halve(p, k + 1)

    outs = [o_outer, o_inner, o_qkv.at[0], o_qkv.at[1], o_qkv.at[2], o_proj]

    def gelu_parts(h):
        k0, k1 = 0.7978845608028654, 0.044715
        sq = h * h
        t = jnp.tanh(k0 * h * (1.0 + k1 * sq))
        active = (0.5 * h * (1.0 + t)).astype(BF)
        return active, 0.5 * (1.0 + t) + 0.5 * h * (1.0 - t * t) * (k0 * (1.0 + 3.0 * k1 * sq))

    def image_active():
        normed, _ = normalize(g_in[1, 0].astype(F32))
        a_more[...] = (normed * gain_mlp[...]).astype(BF)
        for j in range(hid // tile):
            c = slice(j * tile, (j + 1) * tile)
            h = dot(a_more[...], w_inner[:, c]) + bias[:, c]
            r_act[1, :, c], dgelu[:, c] = gelu_parts(h)

    def image_grad():
        for j in range(hid // tile):
            c = slice(j * tile, (j + 1) * tile)
            r_gh[1, :, c] = (dot(g_in[1, 1], w_outer[:, c]) * dgelu[:, c]).astype(BF)

    c_of = ag_start(g_of)
    c_low = ag_start(g_low)
    own = g_in.at[0, :, :, cols(me)]
    swap = send(own, g_in.at[1, :, :, cols(me)], partner[0], me)
    ag_mid(g_of, c_of)
    ag_end(c_of)
    normed, sp_mlp = normalize(g_of[...].astype(F32))
    n_mlp[...] = normed
    a_mlp[...] = (normed * gain_mlp[...]).astype(BF)
    ag_mid(g_low, c_low)

    swap.wait_recv()
    c_1 = ag_start(g_in.at[1])
    weights[0].wait()
    for j in range(hid // tile):
        c = slice(j * tile, (j + 1) * tile)
        h = dot(a_mlp[...], w_inner[:, c]) + bias[:, c]
        r_act[0, :, c], dgelu[:, c] = gelu_parts(h)
    ag_end(c_low)
    weights[1].wait()
    c_mlp = rs_start(0, lambda i: dot(r_act[0], w_outer[cols(i), :], NT))
    for j in range(hid // tile):
        c = slice(j * tile, (j + 1) * tile)
        gl = (dot(g_low[...], w_outer[:, c]) * dgelu[:, c]).astype(BF)
        r_gh[0, :, c] = gl
        sm_s[0, :, 2 * width + j * tile : 2 * width + (j + 1) * tile] = jnp.sum(
            gl.astype(F32), 0, keepdims=True
        )
    rs_mid(0, c_mlp)
    c_gn = rs_start(1, lambda i: dot(r_gh[0], w_inner[cols(i), :], NT))
    ag_mid(g_in.at[1], c_1)
    ag_end(c_1)
    image_active()
    rs_mid(1, c_gn)
    total = rs_end(0, c_mlp)
    second = (os_ref[0].astype(F32) - total[0:length]).astype(BF)
    o_is[0] = second
    g_is[:, cols(me)] = jnp.zeros((rows, width), BF)
    g_is[0:length, cols(me)] = second
    c_is = ag_start(g_is)
    c_gf = ag_start(g_gf)
    keep_left(0, 1, g_low)
    keep_left(1, 1, g_in.at[1, 1])
    zs = [None] * 6
    zs[0] = mlp_piece(0, 1, r_act)
    ag_mid(g_is, c_is)
    total = rs_end(1, c_gn)
    g_gn[:, cols(me)] = total.astype(BF)
    c_ggn = ag_start(g_gn)
    sm_s[0, :, width : 2 * width] = jnp.sum(total * n_mlp[:, cols(me)], 0, keepdims=True)
    image_grad()
    ag_mid(g_gf, c_gf)
    ag_end(c_is)
    normed, spread = normalize(g_is[...].astype(F32))
    n_attn[...] = normed
    sp_attn[...] = jnp.broadcast_to(spread, sp_attn.shape)
    a_attn[...] = (normed * gain_attn[...]).astype(BF)
    x_attn = left(0, a_attn)
    ag_mid(g_gn, c_ggn)
    weights[2].wait()
    for j in range(3):
        c = slice(j * width, (j + 1) * width)
        qkv[:, c] = dot(a_attn[...], w_qkv[j]).astype(BF)
    keep_left(0, 0, a_mlp)
    keep_left(1, 0, a_more)
    zs[1] = mlp_piece(1, 0, r_gh)
    ag_end(c_gf)
    ag_end(c_ggn)

    def means(g, n, gain):
        scaled = g * gain
        return (
            jnp.mean(scaled, -1, keepdims=True),
            jnp.mean(scaled * n, -1, keepdims=True),
        )

    g = g_gn[...].astype(F32)
    first, other = means(g, n_mlp[...], gain_mlp[...])
    back = sp_mlp * (g * gain_mlp[...] - first - n_mlp[...] * other)
    a_back[...] = (g_gf[...].astype(F32) + back).astype(BF)
    o_bf[0] = a_back[0:length, cols(me)]
    weights[3].wait()
    gheads[...] = dot(a_back[...], w_proj[...]).astype(BF)
    x_back = left(1, a_back)
    zs[0] = merge(0, 1, zs[0])

    factor = HEAD**-0.5
    valid = lax.broadcasted_iota(jnp.int32, (rows, rows), 1) < length
    for h in range(width // HEAD):
        c = slice(h * HEAD, (h + 1) * HEAD)
        q = qkv[:, c]
        k = qkv[:, width + h * HEAD : width + (h + 1) * HEAD]
        v = qkv[:, 2 * width + h * HEAD : 2 * width + (h + 1) * HEAD]
        gh = gheads[:, c]
        s = jnp.where(valid, dot(q, k, NT) * factor, -1e30)
        e = jnp.exp(s - jnp.max(s, -1, keepdims=True))
        p = e / jnp.sum(e, -1, keepdims=True)
        low = p.astype(BF)
        r_attn[0, :, c] = dot(low, v).astype(BF)
        gp = dot(gh, v, NT)
        gs = (p * (gp - jnp.sum(gp * p, -1, keepdims=True))).astype(BF)
        r_rows[0, 0, :, c] = (dot(gs, k) * factor).astype(BF)
        r_rows[1, 0, :, c] = (dot(gs, q, TN) * factor).astype(BF)
        r_rows[2, 0, :, c] = dot(low, gh, TN).astype(BF)
    x_r = [right(r_rows.at[2]), right(r_rows.at[1]), right(r_rows.at[0])][::-1]
    x_attn_rows = right(r_attn)
    c_gna = rs_start(
        3,
        lambda i: dot(r_rows[0, 0], w_qkv[0, cols(i), :], NT)
        + dot(r_rows[1, 0], w_qkv[1, cols(i), :], NT)
        + dot(r_rows[2, 0], w_qkv[2, cols(i), :], NT),
    )
    c_out = rs_start(2, lambda i: dot(r_attn[0], w_proj[cols(i), :], NT))
    rs_mid(3, c_gna)
    rs_mid(2, c_out)
    x_attn.wait_recv()
    for p in (4, 3, 2):
        zs[p] = piece(p, 0, r_rows.at[p - 2], x_r[p - 2])
    x_back.wait_recv()
    zs[5] = piece(5, 1, r_attn, x_attn_rows)
    zs[1] = merge(1, 1, zs[1])
    total = rs_end(3, c_gna)
    g_gna[:, cols(me)] = total.astype(BF)
    c_ggna = ag_start(g_gna)
    sm_s[0, :, 0:width] = jnp.sum(total * n_attn[:, cols(me)], 0, keepdims=True)
    c_sm = send(sm_s.at[0], sm_r.at[0], partner[0], me)
    for p in (4, 3, 2, 5):
        zs[p] = merge(p, 1, zs[p])
    total = rs_end(2, c_out)
    o_if[0] = (of_ref[0].astype(F32) - total[0:length]).astype(BF)
    ag_mid(g_gna, c_ggna)
    c_sm.wait_recv()
    sm_s[1] = sm_s[0] + sm_r[0]
    c_sm = send(sm_s.at[1], sm_r.at[1], partner[1], me)
    ag_end(c_ggna)
    first, other = means(g_gna[...].astype(F32), n_attn[...], gain_attn[...])
    back = sp_attn[:, 0:1] * (
        g_gna[:, cols(me)].astype(F32) * gain_attn[:, cols(me)]
        - first
        - n_attn[:, cols(me)] * other
    )
    o_bs[0] = (gs_ref[0].astype(F32) + back[0:length]).astype(BF)
    for k in range(2, bits):
        c_sm.wait_recv()
        sm_s[k] = sm_s[k - 1] + sm_r[k - 1]
        c_sm = send(sm_s.at[k], sm_r.at[k], partner[k], me)
        for p in (0, 1, 4, 3, 2, 5):
            zs[p] = merge(p, k, zs[p])
    c_sm.wait_recv()
    small = sm_s[bits - 1] + sm_r[bits - 1]
    o_ga[...] = small[:, 0:width]
    o_gm[...] = small[:, width : 2 * width]
    o_bias[...] = small[:, 2 * width :]
    for c in pending:
        c.wait_send()


def hand_out(*refs):
    count = (len(refs) - 2) // 3
    source, target, held = refs[:count], refs[count : 2 * count], refs[2 * count : 3 * count]
    first = [pltpu.make_async_copy(source[i], held[i], refs[-2].at[i]) for i in range(count)]
    second = [pltpu.make_async_copy(held[i], target[i], refs[-1].at[i]) for i in range(count)]
    for c in first:
        c.start()
    for c, e in zip(first, second):
        c.wait()
        e.start()
    for e in second:
        e.wait()


def on_device(
    out_first, out_second, grad_first, grad_second, gain_attn, gain_mlp,
    qkv_weight, proj_weight, inner_weight, inner_bias, outer_weight,
):
    images, length, width = out_first.shape
    parts = lax.axis_size("tensor")
    groups = lax.axis_size("dp")
    full = width * parts
    hid = inner_weight.shape[1]
    rows = (length + 15) // 16 * 16
    shard = full // groups
    bits = groups.bit_length() - 1
    sizes = (groups, length, width, full, hid, 256, rows)
    vm = pltpu.VMEM
    half = groups // 2
    scratch = [
        vm((3, full, width), BF), vm((full, width), BF), vm((full, hid), BF), vm((full, hid), BF),
    ]
    scratch += [vm((2, 2, rows, full), BF)] + [vm((rows, full), BF)] * 4
    scratch += [vm((rows, full), BF)] * 4
    scratch += [vm((rows, full), F32)] * 2 + [vm((rows, 128), F32)]
    scratch += [vm((rows, hid), F32), vm((rows, 3 * width), BF), vm((rows, width), BF)]
    scratch += [vm((2, half, 2, shard, rows), BF), vm((2, half, shard, rows), BF)]
    scratch += [vm((2, 2, half, shard, rows), BF), vm((half, 2, shard, rows), BF)]
    scratch += [vm((2, rows, hid), BF), vm((2, rows, hid), BF), vm((2, rows, width), BF), vm((3, 2, rows, width), BF)]
    scratch += [
        vm((4, 2, rows, width), BF), vm((4, 2, rows, width), BF), vm((4, 2, rows, width), F32),
        vm((4, rows, width), BF), vm((4, rows, width), BF),
    ]
    small = 2 * width + hid
    scratch += [vm((bits, 1, small), F32), vm((bits, 1, small), F32)]
    for n in (hid, hid, width, width, width, width):
        m = half
        bufs = []
        for k in range(m.bit_length() - 1):
            bufs += [vm((m // 2, 2, shard, n), F32), vm((m // 2, shard, n), BF), vm((m // 2, shard, n), BF)]
            m //= 2
        scratch.append(bufs)
    scratch += [pltpu.SemaphoreType.DMA((80,)), pltpu.SemaphoreType.DMA((80,)), pltpu.SemaphoreType.DMA((4,))]
    local = jax.ShapeDtypeStruct((images, length, width), BF)
    out_shape = [
        local, local, local, local,
        jax.ShapeDtypeStruct((3, shard, width), F32),
        jax.ShapeDtypeStruct((shard, width), F32),
        jax.ShapeDtypeStruct((shard, hid), F32),
        jax.ShapeDtypeStruct((1, width), F32),
        jax.ShapeDtypeStruct((1, width), F32),
        jax.ShapeDtypeStruct((1, hid), F32),
        jax.ShapeDtypeStruct((shard, hid), F32),
    ]
    v = pl.BlockSpec(memory_space=pltpu.VMEM)
    a = pl.BlockSpec(memory_space=pl.ANY)
    hbm = pl.BlockSpec(memory_space=pltpu.HBM)
    o = pl.pallas_call(
        functools.partial(kernel, sizes),
        out_shape=out_shape,
        in_specs=[v] * 7 + [hbm] * 4,
        out_specs=[v] * 11,
        scratch_shapes=scratch,
        compiler_params=pltpu.CompilerParams(
            collective_id=0, has_side_effects=True, vmem_limit_bytes=LIMIT
        ),
    )(
        out_first, out_second, grad_first, grad_second,
        gain_attn.reshape(1, full), gain_mlp.reshape(1, full), inner_bias.reshape(1, hid),
        jnp.transpose(qkv_weight, (1, 0, 2)), proj_weight, inner_weight, outer_weight,
    )
    o = pl.pallas_call(
        hand_out,
        out_shape=out_shape,
        in_specs=[a] * 11,
        out_specs=[a] * 11,
        scratch_shapes=[vm(x.shape, x.dtype) for x in out_shape]
        + [pltpu.SemaphoreType.DMA((11,)), pltpu.SemaphoreType.DMA((11,))],
        compiler_params=pltpu.CompilerParams(vmem_limit_bytes=LIMIT),
    )(*o)
    return (
        o[0], o[1], o[2], o[3], jnp.transpose(o[4], (1, 0, 2)), o[5], o[6],
        o[9].reshape(hid), o[10], o[7].reshape(width), o[8].reshape(width),
    )


def solution(mesh):
    act = P("dp", None, "tensor")
    in_specs = (
        act, act, act, act, P(), P(), P(None, None, "tensor"), P(None, "tensor"),
        P(None, "tensor"), P("tensor"), P(None, "tensor"),
    )
    out_specs = (
        act, act, act, act, P("dp", None, "tensor"), P("dp", "tensor"), P("dp", "tensor"),
        P("tensor"), P("dp", "tensor"), P("tensor"), P("tensor"),
    )
    return jax.shard_map(
        on_device, mesh=mesh, in_specs=in_specs, out_specs=out_specs, check_vma=False
    )
```

profile of v0, /device:TPU:0, one launch (start us, length us, event | category | flops | bytes accessed | tf_op | source)
XLA Modules:
  0.0 85.4 jit_solution(2577490413156021479)
XLA Ops:
  0.6 82.1 %shard_map.194 = (bf16[1,197,256]{2,1,0:T(8,128)(2,1)}, bf16[1,197,256]{2,1,0:T(8,128)(2,1)}, bf16[1,197,256]{2,1,0:T(8,128)(2,1)}, bf16[1,197,256]{2,1,0:T(8,12...) custom-call(bf16[1,197,256]{2,1,0:T(8,128)(2,1)} %of_ref.1, ...), custom_call_target="tpu_custom_call" | custom-call | tf_op jit(solution)/shard_map/pallas_call | solution.py:443
  82.8 2.6 %shard_map.195 = (bf16[1,197,256]{2,1,0:T(8,128)(2,1)}, bf16[1,197,256]{2,1,0:T(8,128)(2,1)}, bf16[1,197,256]{2,1,0:T(8,128)(2,1)}, bf16[1,197,256]{2,1,0:T(8,12...) custom-call(bf16[1,197,256]{2,1,0:T(8,128)(2,1)} %get-tuple-element., ...), custom_call_target="tpu_custom_call" | custom-call | tf_op jit(solution)/shard_map/pallas_call | solution.py:457
where the time goes:
time: 85.6 us; the launch traced here: 85.4 us
  Pallas kernels  84.7 us (99%)
    pallas_call x1, Pallas kernels, on_device(): pl.pallas_call(functools.partial(kernel, sizes), out_shape=out_shape, in_...  82.1 us
    pallas_call x1, Pallas kernels, on_device(): pl.pallas_call(hand_out, out_shape=out_shape, in_specs=[a] * 11, out_spec...  2.59 us

commit v1 on v0

v1 whole, which is shorter than its diff:
```python
import functools

import jax
import jax.numpy as jnp
from jax import lax
from jax.experimental import pallas as pl
from jax.experimental.pallas import tpu as pltpu
from jax.sharding import PartitionSpec as P

epsilon = 1e-06
HEAD = 64
BF = jnp.bfloat16
F32 = jnp.float32
MESH = pl.DeviceIdType.MESH
LIMIT = 61 * 2**20


def dot(a, b, dims=((1,), (0,))):
    return lax.dot_general(a, b, (dims, ((), ())), preferred_element_type=F32)


NT = ((1,), (1,))
TN = ((0,), (0,))


def kernel(
    sizes,
    of_ref, os_ref, gf_ref, gs_ref, gain_attn, gain_mlp, bias,
    qkv_hbm, proj_hbm, inner_hbm, outer_hbm,
    o_if, o_is, o_bf, o_bs, o_qkv, o_proj, o_inner, o_ga, o_gm, o_bias, o_outer,
    w_qkv, w_proj, w_inner, w_outer,
    g_in, g_is, g_back,
    a_mlp, a_more, a_attn, n_mlp, n_attn,
    dgelu, plain, qkv, gheads, probs, u_mlp, u_attn,
    at, lr, atm, at_tmp,
    r_act, r_gh, r_attn, r_rows,
    rs_s1, rs_r1, rs_k, rs_s2, rs_r2,
    st_s, st_r, sm_s, sm_r,
    *rest,
):
    groups, length, width, full, hid, tile, rows, near = sizes
    bits = groups.bit_length() - 1
    shard = full // groups
    m = groups // 2
    upper = groups // (2 * near)
    block = 2 * shard
    near_bits = near.bit_length() - 1
    pieces = rest[:-3]
    ssem, rsem, wsem = rest[-3:]
    d = lax.axis_index("dp")
    me = lax.axis_index("tensor")
    core, yy = me % 2, me // 2
    tc = yy * 2 + 1 - core
    ty = (1 - yy) * 2 + core
    td = (1 - yy) * 2 + 1 - core
    bit = [(d // 2**k) % 2 for k in range(bits)]
    step = [(1 - 2 * bit[k]) * 2**k for k in range(bits)]
    partner = [d + step[k] for k in range(bits)]
    place = (d // 2) % near

    def peer(r):
        return d + sum(step[1 + k] for k in range(near_bits) if r // 2**k % 2)

    counter = [0]
    pending = []

    def send(src, dst, dp_id, t_id):
        k = counter[0]
        counter[0] += 1
        c = pltpu.make_async_remote_copy(
            src_ref=src, dst_ref=dst, send_sem=ssem.at[k], recv_sem=rsem.at[k],
            device_id=(dp_id, t_id), device_id_type=MESH,
        )
        c.start()
        pending.append(c)
        return c

    def cols(i):
        return pl.ds(pl.multiple_of(i * width, width), width)

    weights = []
    for i, (src, dst) in enumerate(
        [(inner_hbm, w_inner), (outer_hbm, w_outer), (qkv_hbm, w_qkv), (proj_hbm, w_proj)]
    ):
        c = pltpu.make_async_copy(src, dst, wsem.at[i])
        c.start()
        weights.append(c)

    barrier = pltpu.get_barrier_semaphore()
    peers = [(d, tc), (d, ty), (d, td)] + [(p, me) for p in partner]
    peers += [(peer(r), me) for r in range(1, near) if r.bit_count() > 1]
    for to in peers:
        pl.semaphore_signal(barrier, inc=1, device_id=to, device_id_type=MESH)

    def stage(g, src):
        g[:, cols(me)] = jnp.zeros((rows, width), BF)
        g[0:length, cols(me)] = src[0]

    g_of, g_low = g_in.at[0, 0], g_in.at[0, 1]
    stage(g_of, of_ref)
    stage(g_low, gs_ref)
    pl.semaphore_wait(barrier, len(peers))

    def ag_start(g):
        own = g.at[:, cols(me)]
        c2 = send(own, own, d, ty)
        c1 = send(own, own, d, tc)
        return [c1, c2]

    def ag_mid(g, cs):
        cs[1].wait_recv()
        far = g.at[:, cols(ty)]
        cs.append(send(far, far, d, tc))

    def ag_end(cs):
        cs[0].wait_recv()
        cs[2].wait_recv()

    def rs_start(i, part):
        rs_s1[i, 1] = part(td).astype(BF)
        c1 = send(rs_s1.at[i, 1], rs_r1.at[i, 1], d, tc)
        rs_k[i, 1] = part(ty)
        rs_s1[i, 0] = part(tc).astype(BF)
        c0 = send(rs_s1.at[i, 0], rs_r1.at[i, 0], d, tc)
        rs_k[i, 0] = part(me)
        return [c0, c1]

    def rs_mid(i, cs):
        cs[1].wait_recv()
        rs_s2[i] = (rs_k[i, 1] + rs_r1[i, 1].astype(F32)).astype(BF)
        cs.append(send(rs_s2.at[i], rs_r2.at[i], d, ty))

    def rs_end(i, cs):
        cs[0].wait_recv()
        cs[2].wait_recv()
        return rs_k[i, 0] + rs_r1[i, 0].astype(F32) + rs_r2[i].astype(F32)

    lane = lax.broadcasted_iota(jnp.int32, (rows, 128), 1)

    def stats_start(i, first, other):
        both = jnp.where(lane == 0, first, jnp.where(lane == 1, other, 0.0))
        st_s[i] = both.T[0:8]
        return [
            send(st_s.at[i], st_r.at[i, j], d, to) for j, to in enumerate((ty, td, tc))
        ]

    def stats_end(i, cs):
        for c in cs:
            c.wait_recv()
        total = st_s[i] + st_r[i, 0] + st_r[i, 1] + st_r[i, 2]
        both = total.T / full
        return both[:, 0:1], both[:, 1:2]

    def normalize(values):
        centre = values - jnp.mean(values, -1, keepdims=True)
        spread = lax.rsqrt(jnp.mean(centre * centre, -1, keepdims=True) + epsilon)
        return centre * spread, spread

    def two_parts(gain):
        wide = jnp.broadcast_to(gain, (16, full))
        high = wide.astype(BF).astype(F32)
        row = lax.broadcasted_iota(jnp.int32, (16, full), 0)
        return jnp.where(row == 0, high, wide - high).astype(BF)

    def left(i, a):
        at[i] = a[...].T.reshape(m, 2, shard, rows)
        part = pl.ds(core * (m // 2), m // 2)
        return send(at.at[i, part, 1 - bit[0]], lr.at[i, part], partner[0], me)

    def left_mid(i, c):
        c.wait_recv()
        part = pl.ds(core * (m // 2), m // 2)
        return send(lr.at[i, part], lr.at[i, part], d, tc)

    def right(r):
        return send(r.at[0], r.at[1], partner[0], me)

    def piece(p, i, r, cr):
        cr.wait_recv()
        keep = pieces[p][0]
        mine = at[i, :, bit[0]].reshape(m * shard, rows)
        theirs = lr[i].reshape(m * shard, rows)
        acc = dot(mine, r[0]) + dot(theirs, r[1])
        keep[...] = acc.reshape(m // 2, 2, shard, width)
        return halve(p, 0)

    def keep_left(r, kind, a):
        if upper == 1 and block % 128 == 0:
            at_c = pl.ds(pl.multiple_of(place * block, block), block)
            atm[kind, r] = a[:, at_c].T
        else:
            at_tmp[...] = a[...].T.reshape(upper, near, block, rows)
            atm[kind, r] = at_tmp[:, place].reshape(upper * block, rows)

    def mlp_piece(p, kind, x):
        keep = pieces[p][0]
        for j in range(hid // tile):
            c = slice(j * tile, (j + 1) * tile)
            acc = dot(atm[kind, 0], x[0, :, c])
            for r in range(1, near):
                acc = acc + dot(atm[kind, r], x[r, :, c])
            keep[:, :, :, c] = acc.reshape(upper, 2, shard, tile)
        return halve(p, 0)

    far_bits = list(range(1 + near_bits, bits))
    order = [[0] + far_bits] * 2 + [list(range(1, bits))] * 4
    outs = [o_outer, o_inner, o_qkv.at[0], o_qkv.at[1], o_qkv.at[2], o_proj]

    def bufs(p, s):
        return pieces[p][3 * s : 3 * s + 3]

    def halve(p, s):
        keep, out, into = bufs(p, s)
        k = order[p][s]
        out[...] = keep[:, 1 - bit[k]].astype(BF)
        return send(out, into, partner[k], me)

    def merge(p, s, c):
        c.wait_recv()
        keep, out, into = bufs(p, s)
        total = keep[:, bit[order[p][s]]] + into[...].astype(F32)
        if s == len(order[p]) - 1:
            outs[p][...] = total[0]
            return None
        nxt = bufs(p, s + 1)[0]
        nxt[...] = total.reshape(nxt.shape)
        return halve(p, s + 1)

    def gelu_parts(h):
        k0, k1 = 0.7978845608028654, 0.044715
        sq = h * h
        t = jnp.tanh(k0 * h * (1.0 + k1 * sq))
        active = (0.5 * h * (1.0 + t)).astype(BF)
        return active, 0.5 * (1.0 + t) + 0.5 * h * (1.0 - t * t) * (k0 * (1.0 + 3.0 * k1 * sq))

    tiles = [slice(j * tile, (j + 1) * tile) for j in range(hid // tile)]

    def image(r):
        normed, _ = normalize(g_in[r, 0].astype(F32))
        a_more[...] = (normed * gain_mlp[...]).astype(BF)
        keep_left(r, 0, a_more)
        keep_left(r, 1, g_in.at[r, 1])
        for c in tiles:
            h = dot(a_more[...], w_inner[:, c]) + bias[:, c]
            r_act[r, :, c], slope = gelu_parts(h)
            r_gh[r, :, c] = (dot(g_in[r, 1], w_outer[:, c]) * slope).astype(BF)

    c_of = ag_start(g_of)
    c_low = ag_start(g_low)
    own = g_in.at[0, :, :, cols(me)]
    c_z = [None] + [send(own, g_in.at[r, :, :, cols(me)], peer(r), me) for r in range(1, near)]
    weights[0].wait()
    for c in tiles:
        both = dot(two_parts(gain_mlp[...]), w_inner[:, c])
        u_mlp[:, c] = both[0:1] + both[1:2]
    ag_mid(g_of, c_of)
    ag_end(c_of)
    normed, sp_mlp = normalize(g_of[...].astype(F32))
    n_mlp[...] = normed
    a_mlp[...] = (normed * gain_mlp[...]).astype(BF)
    ag_mid(g_low, c_low)
    for c in tiles:
        h = dot(a_mlp[...], w_inner[:, c])
        plain[:, c] = h
        r_act[0, :, c], dgelu[:, c] = gelu_parts(h + bias[:, c])
    weights[1].wait()
    c_mlp = rs_start(0, lambda i: dot(r_act[0], w_outer[cols(i), :], NT))
    ag_end(c_low)
    first = jnp.zeros((rows, 1), F32)
    other = jnp.zeros((rows, 1), F32)
    for c in tiles:
        gl = (dot(g_low[...], w_outer[:, c]) * dgelu[:, c]).astype(BF)
        r_gh[0, :, c] = gl
        gl = gl.astype(F32)
        first = first + jnp.sum(gl * u_mlp[:, c], -1, keepdims=True)
        other = other + jnp.sum(gl * plain[:, c], -1, keepdims=True)
        sm_s[0, :, 2 * width + c.start : 2 * width + c.stop] = jnp.sum(gl, 0, keepdims=True)
    rs_mid(0, c_mlp)
    c_st = stats_start(0, first, other)
    c_gn = rs_start(1, lambda i: dot(r_gh[0], w_inner[cols(i), :], NT))
    keep_left(0, 1, g_low)
    keep_left(0, 0, a_mlp)
    rs_mid(1, c_gn)
    total = rs_end(0, c_mlp)
    second = (os_ref[0].astype(F32) - total[0:length]).astype(BF)
    o_is[0] = second
    g_is[:, cols(me)] = jnp.zeros((rows, width), BF)
    g_is[0:length, cols(me)] = second
    c_is = ag_start(g_is)
    total = rs_end(1, c_gn)
    first, other = stats_end(0, c_st)
    back = sp_mlp * (total * gain_mlp[:, cols(me)] - first - n_mlp[:, cols(me)] * other)
    back = (gf_ref[0].astype(F32) + back[0:length]).astype(BF)
    o_bf[0] = back
    g_back[:, cols(me)] = jnp.zeros((rows, width), BF)
    g_back[0:length, cols(me)] = back
    c_back = ag_start(g_back)
    sm_s[0, :, width : 2 * width] = jnp.sum(total * n_mlp[:, cols(me)], 0, keepdims=True)
    weights[2].wait()
    for j in range(3):
        both = dot(two_parts(gain_attn[...]), w_qkv[j])
        u_attn[j] = both[0:1] + both[1:2]
    ag_mid(g_is, c_is)
    ag_end(c_is)
    normed, sp_attn = normalize(g_is[...].astype(F32))
    n_attn[...] = normed[:, :]
    a_attn[...] = (normed * gain_attn[...]).astype(BF)
    for j in range(3):
        qkv[:, j * width : (j + 1) * width] = dot(a_attn[...], w_qkv[j]).astype(BF)
    factor = HEAD**-0.5
    valid = lax.broadcasted_iota(jnp.int32, (rows, rows), 1) < length
    heads = [slice(h * HEAD, (h + 1) * HEAD) for h in range(width // HEAD)]

    def part_of(j, c):
        return qkv[:, j * width + c.start : j * width + c.stop]

    for h, c in enumerate(heads):
        s = jnp.where(valid, dot(part_of(0, c), part_of(1, c), NT) * factor, -1e30)
        e = jnp.exp(s - jnp.max(s, -1, keepdims=True))
        p = e / jnp.sum(e, -1, keepdims=True)
        probs[h] = p
        r_attn[0, :, c] = dot(p.astype(BF), part_of(2, c)).astype(BF)
    x_attn_rows = right(r_attn)
    x_attn = left(0, a_attn)
    ag_mid(g_back, c_back)
    ag_end(c_back)
    weights[3].wait()
    gheads[...] = dot(g_back[...], w_proj[...]).astype(BF)
    for h, c in enumerate(heads):
        r_rows[2, 0, :, c] = dot(probs[h].astype(BF), gheads[:, c], TN).astype(BF)
    x_v = right(r_rows.at[2])
    x_back = left(1, g_back)
    for h, c in enumerate(heads):
        p = probs[h]
        gp = dot(gheads[:, c], part_of(2, c), NT)
        gs = (p * (gp - jnp.sum(gp * p, -1, keepdims=True))).astype(BF)
        r_rows[0, 0, :, c] = (dot(gs, part_of(1, c)) * factor).astype(BF)
        r_rows[1, 0, :, c] = (dot(gs, part_of(0, c), TN) * factor).astype(BF)
    x_r = [right(r_rows.at[0]), right(r_rows.at[1]), x_v]
    first = jnp.zeros((rows, 1), F32)
    other = jnp.zeros((rows, 1), F32)
    for j in range(3):
        r = r_rows[j, 0].astype(F32)
        first = first + jnp.sum(r * u_attn[j], -1, keepdims=True)
        c = slice(j * width, (j + 1) * width)
        other = other + jnp.sum(r * qkv[:, c].astype(F32), -1, keepdims=True)
    c_gna = rs_start(
        3,
        lambda i: dot(r_rows[0, 0], w_qkv[0, cols(i), :], NT)
        + dot(r_rows[1, 0], w_qkv[1, cols(i), :], NT)
        + dot(r_rows[2, 0], w_qkv[2, cols(i), :], NT),
    )
    c_out = rs_start(2, lambda i: dot(r_attn[0], w_proj[cols(i), :], NT))
    rs_mid(3, c_gna)
    c_st = stats_start(1, first, other)
    rs_mid(2, c_out)
    c_in = [None] * near
    for r in range(1, near):
        c_z[r].wait_recv()
        c_in[r] = [ag_start(g_in.at[r, 0]), ag_start(g_in.at[r, 1])]
    x_attn = left_mid(0, x_attn)
    x_back = left_mid(1, x_back)
    x_back.wait_recv()
    zs = [None] * 6
    zs[5] = piece(5, 1, r_attn, x_attn_rows)
    x_attn.wait_recv()
    zs[4] = piece(4, 0, r_rows.at[2], x_r[2])

    def collect(r):
        for a in range(2):
            ag_mid(g_in.at[r, a], c_in[r][a])
        for a in range(2):
            ag_end(c_in[r][a])
        image(r)

    zs[2] = piece(2, 0, r_rows.at[0], x_r[0])
    zs[3] = piece(3, 0, r_rows.at[1], x_r[1])
    zs[5] = merge(5, 0, zs[5])
    total = rs_end(3, c_gna)
    sm_s[0, :, 0:width] = jnp.sum(total * n_attn[:, cols(me)], 0, keepdims=True)
    c_sm = send(sm_s.at[0], sm_r.at[0], partner[0], me)
    first, other = stats_end(1, c_st)
    back = sp_attn * (
        total * gain_attn[:, cols(me)] - first - n_attn[:, cols(me)] * other
    )
    o_bs[0] = (gs_ref[0].astype(F32) + back[0:length]).astype(BF)
    total = rs_end(2, c_out)
    o_if[0] = (of_ref[0].astype(F32) - total[0:length]).astype(BF)
    zs[4] = merge(4, 0, zs[4])
    for r in range(1, near):
        collect(r)
    zs[0] = mlp_piece(0, 1, r_act)
    zs[1] = mlp_piece(1, 0, r_gh)
    for p in (2, 3):
        zs[p] = merge(p, 0, zs[p])
    for k in range(1, bits):
        c_sm.wait_recv()
        sm_s[k] = sm_s[k - 1] + sm_r[k - 1]
        c_sm = send(sm_s.at[k], sm_r.at[k], partner[k], me)
    for s in range(1, bits - 1):
        for p in (5, 4, 2, 3):
            zs[p] = merge(p, s, zs[p])
    for s in range(len(order[0])):
        for p in (0, 1):
            zs[p] = merge(p, s, zs[p])
    c_sm.wait_recv()
    small = sm_s[bits - 1] + sm_r[bits - 1]
    o_ga[...] = small[:, 0:width]
    o_gm[...] = small[:, width : 2 * width]
    o_bias[...] = small[:, 2 * width :]
    for c in pending:
        c.wait_send()


def hand_out(*refs):
    count = (len(refs) - 2) // 3
    source, target, held = refs[:count], refs[count : 2 * count], refs[2 * count : 3 * count]
    first = [pltpu.make_async_copy(source[i], held[i], refs[-2].at[i]) for i in range(count)]
    second = [pltpu.make_async_copy(held[i], target[i], refs[-1].at[i]) for i in range(count)]
    for c in first:
        c.start()
    for c, e in zip(first, second):
        c.wait()
        e.start()
    for e in second:
        e.wait()


def on_device(
    out_first, out_second, grad_first, grad_second, gain_attn, gain_mlp,
    qkv_weight, proj_weight, inner_weight, inner_bias, outer_weight,
):
    images, length, width = out_first.shape
    parts = lax.axis_size("tensor")
    groups = lax.axis_size("dp")
    full = width * parts
    hid = inner_weight.shape[1]
    rows = (length + 15) // 16 * 16
    shard = full // groups
    bits = groups.bit_length() - 1
    near = min(groups // 2, 4)
    sizes = (groups, length, width, full, hid, 256, rows, near)
    vm = pltpu.VMEM
    half = groups // 2
    upper = groups // (2 * near)
    block = 2 * shard
    scratch = [
        vm((3, full, width), BF), vm((full, width), BF), vm((full, hid), BF), vm((full, hid), BF),
    ]
    scratch += [vm((near, 2, rows, full), BF)] + [vm((rows, full), BF)] * 2
    scratch += [vm((rows, full), BF)] * 3
    scratch += [vm((rows, full), F32)] * 2
    scratch += [vm((rows, hid), F32), vm((rows, hid), F32), vm((rows, 3 * width), BF), vm((rows, width), BF)]
    scratch += [vm((width // HEAD, rows, rows), F32), vm((1, hid), F32), vm((3, 1, width), F32)]
    scratch += [vm((2, half, 2, shard, rows), BF), vm((2, half, shard, rows), BF)]
    scratch += [vm((2, near, upper * block, rows), BF), vm((upper, near, block, rows), BF)]
    scratch += [vm((near, rows, hid), BF), vm((near, rows, hid), BF), vm((2, rows, width), BF), vm((3, 2, rows, width), BF)]
    scratch += [
        vm((4, 2, rows, width), BF), vm((4, 2, rows, width), BF), vm((4, 2, rows, width), F32),
        vm((4, rows, width), BF), vm((4, rows, width), BF),
    ]
    scratch += [vm((2, 8, rows), F32), vm((2, 3, 8, rows), F32)]
    small = 2 * width + hid
    scratch += [vm((bits, 1, small), F32), vm((bits, 1, small), F32)]
    for n, k in ((hid, upper), (hid, upper)) + ((width, half // 2),) * 4:
        bufs = []
        while k >= 1:
            bufs += [vm((k, 2, shard, n), F32), vm((k, shard, n), BF), vm((k, shard, n), BF)]
            k //= 2
        scratch.append(bufs)
    scratch += [pltpu.SemaphoreType.DMA((120,)), pltpu.SemaphoreType.DMA((120,)), pltpu.SemaphoreType.DMA((4,))]
    local = jax.ShapeDtypeStruct((images, length, width), BF)
    out_shape = [
        local, local, local, local,
        jax.ShapeDtypeStruct((3, shard, width), F32),
        jax.ShapeDtypeStruct((shard, width), F32),
        jax.ShapeDtypeStruct((shard, hid), F32),
        jax.ShapeDtypeStruct((1, width), F32),
        jax.ShapeDtypeStruct((1, width), F32),
        jax.ShapeDtypeStruct((1, hid), F32),
        jax.ShapeDtypeStruct((shard, hid), F32),
    ]
    v = pl.BlockSpec(memory_space=pltpu.VMEM)
    a = pl.BlockSpec(memory_space=pl.ANY)
    hbm = pl.BlockSpec(memory_space=pltpu.HBM)
    o = pl.pallas_call(
        functools.partial(kernel, sizes),
        out_shape=out_shape,
        in_specs=[v] * 7 + [hbm] * 4,
        out_specs=[v] * 11,
        scratch_shapes=scratch,
        compiler_params=pltpu.CompilerParams(
            collective_id=0, has_side_effects=True, vmem_limit_bytes=LIMIT
        ),
    )(
        out_first, out_second, grad_first, grad_second,
        gain_attn.reshape(1, full), gain_mlp.reshape(1, full), inner_bias.reshape(1, hid),
        jnp.transpose(qkv_weight, (1, 0, 2)), proj_weight, inner_weight, outer_weight,
    )
    o = pl.pallas_call(
        hand_out,
        out_shape=out_shape,
        in_specs=[a] * 11,
        out_specs=[a] * 11,
        scratch_shapes=[vm(x.shape, x.dtype) for x in out_shape]
        + [pltpu.SemaphoreType.DMA((11,)), pltpu.SemaphoreType.DMA((11,))],
        compiler_params=pltpu.CompilerParams(vmem_limit_bytes=LIMIT),
    )(*o)
    return (
        o[0], o[1], o[2], o[3], jnp.transpose(o[4], (1, 0, 2)), o[5], o[6],
        o[9].reshape(hid), o[10], o[7].reshape(width), o[8].reshape(width),
    )


def solution(mesh):
    act = P("dp", None, "tensor")
    in_specs = (
        act, act, act, act, P(), P(), P(None, None, "tensor"), P(None, "tensor"),
        P(None, "tensor"), P("tensor"), P(None, "tensor"),
    )
    out_specs = (
        act, act, act, act, P("dp", None, "tensor"), P("dp", "tensor"), P("dp", "tensor"),
        P("tensor"), P("dp", "tensor"), P("tensor"), P("tensor"),
    )
    return jax.shard_map(
        on_device, mesh=mesh, in_specs=in_specs, out_specs=out_specs, check_vma=False
    )
```

time: 85.6 us -> 79.8 us (0.932)
  Pallas kernels: 84.7 us -> 78.7 us
    pallas_call x1, Pallas kernels: 82.1 us -> 76.1 us  [on_device(): pl.pallas_call(functools.partial(kernel, sizes), out_shape=out_shape, in_...]
where the time goes in v1:
time: 79.8 us; the launch traced here: 79.5 us
  Pallas kernels  78.7 us (99%)
  between operations  0.82 us (1%)
    pallas_call x1, Pallas kernels, on_device(): pl.pallas_call(functools.partial(kernel, sizes), out_shape=out_shape, in_...  76.1 us
    pallas_call x1, Pallas kernels, on_device(): pl.pallas_call(hand_out, out_shape=out_shape, in_specs=[a] * 11, out_spec...  2.59 us

profile of v1, /device:TPU:0, one launch (start us, length us, event | category | flops | bytes accessed | tf_op | source)
XLA Modules:
  0.0 79.5 jit_solution(11754705030057718445)
XLA Ops:
  0.6 76.1 %shard_map.194 = (bf16[1,197,256]{2,1,0:T(8,128)(2,1)}, bf16[1,197,256]{2,1,0:T(8,128)(2,1)}, bf16[1,197,256]{2,1,0:T(8,128)(2,1)}, bf16[1,197,256]{2,1,0:T(8,12...) custom-call(bf16[1,197,256]{2,1,0:T(8,128)(2,1)} %of_ref.1, ...), custom_call_target="tpu_custom_call" | custom-call | tf_op jit(solution)/shard_map/pallas_call | solution.py:486
  76.7 2.6 %shard_map.195 = (bf16[1,197,256]{2,1,0:T(8,128)(2,1)}, bf16[1,197,256]{2,1,0:T(8,128)(2,1)}, bf16[1,197,256]{2,1,0:T(8,128)(2,1)}, bf16[1,197,256]{2,1,0:T(8,12...) custom-call(bf16[1,197,256]{2,1,0:T(8,128)(2,1)} %get-tuple-element., ...), custom_call_target="tpu_custom_call" | custom-call | tf_op jit(solution)/shard_map/pallas_call | solution.py:500

commit v2 on v1

--- a/solution.py
+++ b/solution.py
@@ -32,7 +32,7 @@
     g_in, g_is, g_back,
     a_mlp, a_more, a_attn, n_mlp, n_attn,
     dgelu, plain, qkv, gheads, probs, u_mlp, u_attn,
-    at, lr, atm, at_tmp,
+    own_t, their_t, ls, lr, pt_s, pt_r, spare, atm, at_tmp,
     r_act, r_gh, r_attn, r_rows,
     rs_s1, rs_r1, rs_k, rs_s2, rs_r2,
     st_s, st_r, sm_s, sm_r,
@@ -42,6 +42,7 @@
     bits = groups.bit_length() - 1
     shard = full // groups
     m = groups // 2
+    mine = m * width // full
     upper = groups // (2 * near)
     block = 2 * shard
     near_bits = near.bit_length() - 1
@@ -101,15 +102,15 @@
     stage(g_low, gs_ref)
     pl.semaphore_wait(barrier, len(peers))
 
-    def ag_start(g):
-        own = g.at[:, cols(me)]
+    def ag_start(view):
+        own = view(me)
         c2 = send(own, own, d, ty)
         c1 = send(own, own, d, tc)
         return [c1, c2]
 
-    def ag_mid(g, cs):
+    def ag_mid(view, cs):
         cs[1].wait_recv()
-        far = g.at[:, cols(ty)]
+        far = view(ty)
         cs.append(send(far, far, d, tc))
 
     def ag_end(cs):
@@ -137,9 +138,12 @@
 
     lane = lax.broadcasted_iota(jnp.int32, (rows, 128), 1)
 
+    def as_rows(first, other):
+        both = jnp.where(lane == 0, first, jnp.where(lane == 1, other, 0.0))
+        return both.T[0:8]
+
     def stats_start(i, first, other):
-        both = jnp.where(lane == 0, first, jnp.where(lane == 1, other, 0.0))
-        st_s[i] = both.T[0:8]
+        st_s[i] = as_rows(first, other)
         return [
             send(st_s.at[i], st_r.at[i, j], d, to) for j, to in enumerate((ty, td, tc))
         ]
@@ -152,9 +156,10 @@
         return both[:, 0:1], both[:, 1:2]
 
     def normalize(values):
-        centre = values - jnp.mean(values, -1, keepdims=True)
+        mean = jnp.mean(values, -1, keepdims=True)
+        centre = values - mean
         spread = lax.rsqrt(jnp.mean(centre * centre, -1, keepdims=True) + epsilon)
-        return centre * spread, spread
+        return centre * spread, spread, mean
 
     def two_parts(gain):
         wide = jnp.broadcast_to(gain, (16, full))
@@ -162,15 +167,39 @@
         row = lax.broadcasted_iota(jnp.int32, (16, full), 0)
         return jnp.where(row == 0, high, wide - high).astype(BF)
 
-    def left(i, a):
-        at[i] = a[...].T.reshape(m, 2, shard, rows)
-        part = pl.ds(core * (m // 2), m // 2)
-        return send(at.at[i, part, 1 - bit[0]], lr.at[i, part], partner[0], me)
-
-    def left_mid(i, c):
-        c.wait_recv()
-        part = pl.ds(core * (m // 2), m // 2)
-        return send(lr.at[i, part], lr.at[i, part], d, tc)
+    def pick(values, parity):
+        if mine == 1:
+            return jnp.where(parity == 0, values[:, :shard], values[:, shard:])
+        t = values.T.reshape(mine, 2, shard, values.shape[0])
+        t = jnp.where(parity == 0, t[:, 0], t[:, 1])
+        return t.reshape(mine * shard, values.shape[0]).T
+
+    def share(i, a):
+        ls[i] = pick(a[:, cols(me)], 1 - bit[0])
+        return send(ls.at[i], lr.at[i, me], partner[0], me)
+
+    def shared(i):
+        return lambda t: lr.at[i, t]
+
+    def keep_theirs(i, moments=None):
+        n = mine * shard
+        for t in range(full // width):
+            a = lr[i, t]
+            if moments is not None:
+                mean, spread = moments
+                gain = jnp.broadcast_to(gain_attn[:, t * width : (t + 1) * width], (16, width))
+                gain = pick(gain, bit[0])[0:1]
+                a = ((a.astype(F32) - mean) * spread * gain).astype(BF)
+            their_t[i, t * n : (t + 1) * n] = a.T
+
+    def keep_own(i, a):
+        if shard % 128 == 0:
+            for j in range(m):
+                at_c = pl.ds(pl.multiple_of((2 * j + bit[0]) * shard, shard), shard)
+                own_t[i, j] = a[:, at_c].T
+        else:
+            spare[...] = a[...].T.reshape(m, 2, shard, rows)
+            own_t[i] = spare[:, bit[0]]
 
     def right(r):
         return send(r.at[0], r.at[1], partner[0], me)
@@ -178,9 +207,8 @@
     def piece(p, i, r, cr):
         cr.wait_recv()
         keep = pieces[p][0]
-        mine = at[i, :, bit[0]].reshape(m * shard, rows)
-        theirs = lr[i].reshape(m * shard, rows)
-        acc = dot(mine, r[0]) + dot(theirs, r[1])
+        ours = own_t[i].reshape(m * shard, rows)
+        acc = dot(ours, r[0]) + dot(their_t[i], r[1])
         keep[...] = acc.reshape(m // 2, 2, shard, width)
         return halve(p, 0)
 
@@ -236,7 +264,7 @@
     tiles = [slice(j * tile, (j + 1) * tile) for j in range(hid // tile)]
 
     def image(r):
-        normed, _ = normalize(g_in[r, 0].astype(F32))
+        normed, _, _ = normalize(g_in[r, 0].astype(F32))
         a_more[...] = (normed * gain_mlp[...]).astype(BF)
         keep_left(r, 0, a_more)
         keep_left(r, 1, g_in.at[r, 1])
@@ -245,26 +273,44 @@
             r_act[r, :, c], slope = gelu_parts(h)
             r_gh[r, :, c] = (dot(g_in[r, 1], w_outer[:, c]) * slope).astype(BF)
 
-    c_of = ag_start(g_of)
-    c_low = ag_start(g_low)
-    own = g_in.at[0, :, :, cols(me)]
-    c_z = [None] + [send(own, g_in.at[r, :, :, cols(me)], peer(r), me) for r in range(1, near)]
+    def whole_rows(g):
+        return lambda t: g.at[:, cols(t)]
+
+    def one_of(r, a):
+        return whole_rows(g_in.at[r, a])
+
+    def both_of(r):
+        return lambda t: g_in.at[r, :, :, cols(t)]
+
+    by_tensor = [r for r in (3, 2) if r < near]
+    by_near = [1] if near > 1 else []
+    v_of, v_low, v_is, v_back = map(whole_rows, (g_of, g_low, g_is, g_back))
+    c_of = ag_start(v_of)
+    c_z = [None] * near
+    for r in by_near + by_tensor[:1]:
+        c_z[r] = send(both_of(0)(me), both_of(r)(me), peer(r), me)
     weights[0].wait()
     for c in tiles:
         both = dot(two_parts(gain_mlp[...]), w_inner[:, c])
         u_mlp[:, c] = both[0:1] + both[1:2]
-    ag_mid(g_of, c_of)
+    c_low = ag_start(v_low)
+    ag_mid(v_of, c_of)
     ag_end(c_of)
-    normed, sp_mlp = normalize(g_of[...].astype(F32))
+    normed, sp_mlp, _ = normalize(g_of[...].astype(F32))
     n_mlp[...] = normed
     a_mlp[...] = (normed * gain_mlp[...]).astype(BF)
-    ag_mid(g_low, c_low)
+    ag_mid(v_low, c_low)
+    c_far = {r: send(both_of(0)(ty), both_of(r)(ty), peer(r), me) for r in by_near}
+    for r in by_tensor[1:]:
+        c_z[r] = send(both_of(0)(me), both_of(r)(me), peer(r), me)
+        c_far[r] = send(v_of(ty), one_of(r, 0)(ty), peer(r), me)
     for c in tiles:
         h = dot(a_mlp[...], w_inner[:, c])
         plain[:, c] = h
         r_act[0, :, c], dgelu[:, c] = gelu_parts(h + bias[:, c])
     weights[1].wait()
     c_mlp = rs_start(0, lambda i: dot(r_act[0], w_outer[cols(i), :], NT))
+    rs_mid(0, c_mlp)
     ag_end(c_low)
     first = jnp.zeros((rows, 1), F32)
     other = jnp.zeros((rows, 1), F32)
@@ -275,18 +321,22 @@
         first = first + jnp.sum(gl * u_mlp[:, c], -1, keepdims=True)
         other = other + jnp.sum(gl * plain[:, c], -1, keepdims=True)
         sm_s[0, :, 2 * width + c.start : 2 * width + c.stop] = jnp.sum(gl, 0, keepdims=True)
-    rs_mid(0, c_mlp)
+    c_gn = rs_start(1, lambda i: dot(r_gh[0], w_inner[cols(i), :], NT))
     c_st = stats_start(0, first, other)
-    c_gn = rs_start(1, lambda i: dot(r_gh[0], w_inner[cols(i), :], NT))
+    rs_mid(1, c_gn)
     keep_left(0, 1, g_low)
     keep_left(0, 0, a_mlp)
-    rs_mid(1, c_gn)
     total = rs_end(0, c_mlp)
     second = (os_ref[0].astype(F32) - total[0:length]).astype(BF)
     o_is[0] = second
     g_is[:, cols(me)] = jnp.zeros((rows, width), BF)
     g_is[0:length, cols(me)] = second
-    c_is = ag_start(g_is)
+    c_is = ag_start(v_is)
+    x_attn = share(0, g_is)
+    weights[2].wait()
+    for j in range(3):
+        both = dot(two_parts(gain_attn[...]), w_qkv[j])
+        u_attn[j] = both[0:1] + both[1:2]
     total = rs_end(1, c_gn)
     first, other = stats_end(0, c_st)
     back = sp_mlp * (total * gain_mlp[:, cols(me)] - first - n_mlp[:, cols(me)] * other)
@@ -294,17 +344,26 @@
     o_bf[0] = back
     g_back[:, cols(me)] = jnp.zeros((rows, width), BF)
     g_back[0:length, cols(me)] = back
-    c_back = ag_start(g_back)
+    c_back = ag_start(v_back)
+    x_back = share(1, g_back)
     sm_s[0, :, width : 2 * width] = jnp.sum(total * n_mlp[:, cols(me)], 0, keepdims=True)
-    weights[2].wait()
-    for j in range(3):
-        both = dot(two_parts(gain_attn[...]), w_qkv[j])
-        u_attn[j] = both[0:1] + both[1:2]
-    ag_mid(g_is, c_is)
+    ag_mid(v_is, c_is)
     ag_end(c_is)
-    normed, sp_attn = normalize(g_is[...].astype(F32))
-    n_attn[...] = normed[:, :]
+    c_in = {}
+
+    def forward(view, t, c):
+        c.wait_recv()
+        return send(view(t), view(t), d, tc)
+
+    x_attn.wait_recv()
+    x_attn = ag_start(shared(0))
+    for r in by_near:
+        c_in[r] = [forward(both_of(r), me, c_z[r])]
+    normed, sp_attn, mean = normalize(g_is[...].astype(F32))
+    n_attn[...] = normed
     a_attn[...] = (normed * gain_attn[...]).astype(BF)
+    pt_s[...] = as_rows(mean, sp_attn)
+    c_pt = send(pt_s, pt_r, partner[0], me)
     for j in range(3):
         qkv[:, j * width : (j + 1) * width] = dot(a_attn[...], w_qkv[j]).astype(BF)
     factor = HEAD**-0.5
@@ -321,15 +380,22 @@
         probs[h] = p
         r_attn[0, :, c] = dot(p.astype(BF), part_of(2, c)).astype(BF)
     x_attn_rows = right(r_attn)
-    x_attn = left(0, a_attn)
-    ag_mid(g_back, c_back)
+    x_back.wait_recv()
+    x_back = ag_start(shared(1))
+    for r in by_tensor[:1]:
+        c_z[r].wait_recv()
+        c_in[r] = ag_start(both_of(r))
+    ag_mid(v_back, c_back)
     ag_end(c_back)
+    for r in by_tensor[1:]:
+        c_z[r].wait_recv()
+        c_in[r] = ag_start(one_of(r, 1))
+        c_in[r].append(send(one_of(r, 0)(me), one_of(r, 0)(me), d, tc))
     weights[3].wait()
     gheads[...] = dot(g_back[...], w_proj[...]).astype(BF)
     for h, c in enumerate(heads):
         r_rows[2, 0, :, c] = dot(probs[h].astype(BF), gheads[:, c], TN).astype(BF)
     x_v = right(r_rows.at[2])
-    x_back = left(1, g_back)
     for h, c in enumerate(heads):
         p = probs[h]
         gp = dot(gheads[:, c], part_of(2, c), NT)
@@ -337,6 +403,63 @@
         r_rows[0, 0, :, c] = (dot(gs, part_of(1, c)) * factor).astype(BF)
         r_rows[1, 0, :, c] = (dot(gs, part_of(0, c), TN) * factor).astype(BF)
     x_r = [right(r_rows.at[0]), right(r_rows.at[1]), x_v]
+    for r in by_near:
+        c_in[r].append(forward(both_of(r), ty, c_far[r]))
+    c_gna = rs_start(
+        3,
+        lambda i: dot(r_rows[0, 0], w_qkv[0, cols(i), :], NT)
+        + dot(r_rows[1, 0], w_qkv[1, cols(i), :], NT)
+        + dot(r_rows[2, 0], w_qkv[2, cols(i), :], NT),
+    )
+    ag_mid(shared(0), x_attn)
+    ag_mid(shared(1), x_back)
+    for r in by_near:
+        for c in c_in[r]:
+            c.wait_recv()
+        image(r)
+    rs_mid(3, c_gna)
+    zs = [None] * 6
+    keep_own(1, g_back)
+    ag_end(x_back)
+    keep_theirs(1)
+    zs[5] = piece(5, 1, r_attn, x_attn_rows)
+    keep_own(0, a_attn)
+    c_pt.wait_recv()
+    moments = pt_r[...].T
+    ag_end(x_attn)
+    keep_theirs(0, (moments[:, 0:1], moments[:, 1:2]))
+    for r in by_tensor[:1]:
+        ag_mid(both_of(r), c_in[r])
+    zs[4] = piece(4, 0, r_rows.at[2], x_r[2])
+    for r in by_tensor[1:]:
+        c_in[r].append(forward(one_of(r, 0), ty, c_far[r]))
+    for r in by_tensor[:1]:
+        ag_end(c_in[r])
+        image(r)
+    zs[2] = piece(2, 0, r_rows.at[0], x_r[0])
+    for r in by_tensor[1:]:
+        cs = c_in[r]
+        ag_mid(one_of(r, 1), cs)
+    zs[3] = piece(3, 0, r_rows.at[1], x_r[1])
+    total = rs_end(3, c_gna)
+    sm_s[0, :, 0:width] = jnp.sum(total * n_attn[:, cols(me)], 0, keepdims=True)
+    c_sm = send(sm_s.at[0], sm_r.at[0], partner[0], me)
+    for r in by_tensor[1:]:
+        for i in (0, 2, 3, 4):
+            c_in[r][i].wait_recv()
+        image(r)
+    zs[0] = mlp_piece(0, 1, r_act)
+    zs[1] = mlp_piece(1, 0, r_gh)
+
+    def small_step(k):
+        c_sm.wait_recv()
+        sm_s[k] = sm_s[k - 1] + sm_r[k - 1]
+        return send(sm_s.at[k], sm_r.at[k], partner[k], me)
+
+    c_sm = small_step(1)
+    zs[5] = merge(5, 0, zs[5])
+    zs[4] = merge(4, 0, zs[4])
+    c_out = rs_start(2, lambda i: dot(r_attn[0], w_proj[cols(i), :], NT))
     first = jnp.zeros((rows, 1), F32)
     other = jnp.zeros((rows, 1), F32)
     for j in range(3):
@@ -344,41 +467,10 @@
         first = first + jnp.sum(r * u_attn[j], -1, keepdims=True)
         c = slice(j * width, (j + 1) * width)
         other = other + jnp.sum(r * qkv[:, c].astype(F32), -1, keepdims=True)
-    c_gna = rs_start(
-        3,
-        lambda i: dot(r_rows[0, 0], w_qkv[0, cols(i), :], NT)
-        + dot(r_rows[1, 0], w_qkv[1, cols(i), :], NT)
-        + dot(r_rows[2, 0], w_qkv[2, cols(i), :], NT),
-    )
-    c_out = rs_start(2, lambda i: dot(r_attn[0], w_proj[cols(i), :], NT))
-    rs_mid(3, c_gna)
     c_st = stats_start(1, first, other)
     rs_mid(2, c_out)
-    c_in = [None] * near
-    for r in range(1, near):
-        c_z[r].wait_recv()
-        c_in[r] = [ag_start(g_in.at[r, 0]), ag_start(g_in.at[r, 1])]
-    x_attn = left_mid(0, x_attn)
-    x_back = left_mid(1, x_back)
-    x_back.wait_recv()
-    zs = [None] * 6
-    zs[5] = piece(5, 1, r_attn, x_attn_rows)
-    x_attn.wait_recv()
-    zs[4] = piece(4, 0, r_rows.at[2], x_r[2])
-
-    def collect(r):
-        for a in range(2):
-            ag_mid(g_in.at[r, a], c_in[r][a])
-        for a in range(2):
-            ag_end(c_in[r][a])
-        image(r)
-
-    zs[2] = piece(2, 0, r_rows.at[0], x_r[0])
-    zs[3] = piece(3, 0, r_rows.at[1], x_r[1])
-    zs[5] = merge(5, 0, zs[5])
-    total = rs_end(3, c_gna)
-    sm_s[0, :, 0:width] = jnp.sum(total * n_attn[:, cols(me)], 0, keepdims=True)
-    c_sm = send(sm_s.at[0], sm_r.at[0], partner[0], me)
+    zs[2] = merge(2, 0, zs[2])
+    zs[3] = merge(3, 0, zs[3])
     first, other = stats_end(1, c_st)
     back = sp_attn * (
         total * gain_attn[:, cols(me)] - first - n_attn[:, cols(me)] * other
@@ -386,17 +478,8 @@
     o_bs[0] = (gs_ref[0].astype(F32) + back[0:length]).astype(BF)
     total = rs_end(2, c_out)
     o_if[0] = (of_ref[0].astype(F32) - total[0:length]).astype(BF)
-    zs[4] = merge(4, 0, zs[4])
-    for r in range(1, near):
-        collect(r)
-    zs[0] = mlp_piece(0, 1, r_act)
-    zs[1] = mlp_piece(1, 0, r_gh)
-    for p in (2, 3):
-        zs[p] = merge(p, 0, zs[p])
-    for k in range(1, bits):
-        c_sm.wait_recv()
-        sm_s[k] = sm_s[k - 1] + sm_r[k - 1]
-        c_sm = send(sm_s.at[k], sm_r.at[k], partner[k], me)
+    for k in range(2, bits):
+        c_sm = small_step(k)
     for s in range(1, bits - 1):
         for p in (5, 4, 2, 3):
             zs[p] = merge(p, s, zs[p])
@@ -452,7 +535,10 @@
     scratch += [vm((rows, full), F32)] * 2
     scratch += [vm((rows, hid), F32), vm((rows, hid), F32), vm((rows, 3 * width), BF), vm((rows, width), BF)]
     scratch += [vm((width // HEAD, rows, rows), F32), vm((1, hid), F32), vm((3, 1, width), F32)]
-    scratch += [vm((2, half, 2, shard, rows), BF), vm((2, half, shard, rows), BF)]
+    mine = half // parts
+    scratch += [vm((2, half, shard, rows), BF), vm((2, half * shard, rows), BF)]
+    scratch += [vm((2, rows, mine * shard), BF), vm((2, parts, rows, mine * shard), BF)]
+    scratch += [vm((8, rows), F32), vm((8, rows), F32), vm((half, 2, shard, rows), BF)]
     scratch += [vm((2, near, upper * block, rows), BF), vm((upper, near, block, rows), BF)]
     scratch += [vm((near, rows, hid), BF), vm((near, rows, hid), BF), vm((2, rows, width), BF), vm((3, 2, rows, width), BF)]
     scratch += [

time: 79.8 us -> 64.1 us (0.80)
  Pallas kernels: 78.7 us -> 63.1 us
    pallas_call x1, Pallas kernels: 76.1 us -> 60.5 us  [on_device(): pl.pallas_call(functools.partial(kernel, sizes), out_shape=out_shape, in_...]
where the time goes in v2:
time: 64.1 us; the launch traced here: 63.9 us
  Pallas kernels  63.1 us (98%)
  between operations  0.82 us (1%)
    pallas_call x1, Pallas kernels, on_device(): pl.pallas_call(functools.partial(kernel, sizes), out_shape=out_shape, in_...  60.5 us
    pallas_call x1, Pallas kernels, on_device(): pl.pallas_call(hand_out, out_shape=out_shape, in_specs=[a] * 11, out_spec...  2.59 us

profile of v2, /device:TPU:0, one launch (start us, length us, event | category | flops | bytes accessed | tf_op | source)
XLA Modules:
  0.0 63.9 jit_solution(2692065915219096120)
XLA Ops:
  0.6 60.5 %shard_map.194 = (bf16[1,197,256]{2,1,0:T(8,128)(2,1)}, bf16[1,197,256]{2,1,0:T(8,128)(2,1)}, bf16[1,197,256]{2,1,0:T(8,128)(2,1)}, bf16[1,197,256]{2,1,0:T(8,12...) custom-call(bf16[1,197,256]{2,1,0:T(8,128)(2,1)} %of_ref.1, ...), custom_call_target="tpu_custom_call" | custom-call | tf_op jit(solution)/shard_map/pallas_call | solution.py:572
  61.1 2.6 %shard_map.195 = (bf16[1,197,256]{2,1,0:T(8,128)(2,1)}, bf16[1,197,256]{2,1,0:T(8,128)(2,1)}, bf16[1,197,256]{2,1,0:T(8,128)(2,1)}, bf16[1,197,256]{2,1,0:T(8,12...) custom-call(bf16[1,197,256]{2,1,0:T(8,128)(2,1)} %get-tuple-element., ...), custom_call_target="tpu_custom_call" | custom-call | tf_op jit(solution)/shard_map/pallas_call | solution.py:586
